TPU v7x, 32 devices: a whole 2x2x4 slice. The times are simulated.
32 devices in a mesh: seq: 16 (over z, y, core), ch: 2 (over x).
Axes of the slice: x: 2, y: 2, z: 4, core: 2. Of those that a mesh axis runs over, the one named last changes fastest.
Arguments:
- query_gate: bfloat16 [2, 2048, 2048], P('ch', 'seq'), may hold values from -6 to 6
- key_input: bfloat16 [2, 2048, 2048], P('ch', 'seq'), may hold values from -6 to 6
- value_input: bfloat16 [2, 2048, 2048], P('ch', 'seq'), may hold values from -6 to 6
- grad_output: bfloat16 [2, 2048, 2048], P('ch', 'seq'), may hold values from -6 to 6
- filter_raw: bfloat16 [2048, 2048], P('seq'), may hold values from -6 to 6
- skip_gain: float32 [2048], replicated, may hold values from 0.5 to 1.5
Outputs:
- grad_query: bfloat16 [2, 2048, 2048], P('ch', 'seq')
- grad_key: bfloat16 [2, 2048, 2048], P('ch', 'seq')
- grad_value: bfloat16 [2, 2048, 2048], P('ch', 'seq')
- grad_filter: float32 [2048, 2048], P('seq', 'ch')
All inputs are finite; a program needn't handle non-finite values.
Results may differ from a plain program's by a relative error of at most 0.001.
Values sent between devices are 32-bit elements; how exact they have to be, the bound alone decides.
A program may use at most 128 MiB of HBM per device.

v0:
```python
import math

import numpy as np

import jax
import jax.numpy as jnp
from jax import lax
from jax.experimental import pallas as pl
from jax.experimental.pallas import tpu as pltpu
from jax.sharding import PartitionSpec as P


def angle_table(row_index, col_index, modulus):
    turn_count = row_index[:, None] * col_index[None, :] % modulus
    angles = turn_count.astype(jnp.float32) * (2.0 * math.pi / modulus)
    return (jnp.cos(angles), jnp.sin(angles))


def contract(pattern, table, operand):
    return jnp.einsum(
        pattern, table, operand, precision=lax.Precision.HIGHEST, preferred_element_type=jnp.float32
    )


def rotate(pattern, cos_table, sin_table, sense_sign, real_part, imag_part, want_imag):
    if imag_part is None:
        cos_term = contract(pattern, cos_table, real_part)
        return (cos_term, sense_sign * contract(pattern, sin_table, real_part))
    real_out = contract(pattern, cos_table, real_part) - sense_sign * contract(
        pattern, sin_table, imag_part
    )
    if not want_imag:
        return (real_out, None)
    imag_out = contract(pattern, cos_table, imag_part) + sense_sign * contract(
        pattern, sin_table, real_part
    )
    return (real_out, imag_out)


def twist(cos_table, sin_table, sense_sign, real_part, imag_part):
    return (
        real_part * cos_table - sense_sign * imag_part * sin_table,
        imag_part * cos_table + sense_sign * real_part * sin_table,
    )


def spectral_terms(z_real, z_imag, g_real, g_imag, h_real, h_imag):
    conv_real = z_real * h_real - z_imag * h_imag
    conv_imag = z_real * h_imag + z_imag * h_real
    back_real = h_real * g_real + h_imag * g_imag
    back_imag = h_real * g_imag - h_imag * g_real
    corr_real = z_real * g_real + z_imag * g_imag
    corr_imag = z_real * g_imag - z_imag * g_real
    return (conv_real - back_imag, conv_imag + back_real, corr_real, corr_imag)


def shards(query_gate, key_input, value_input, grad_output, filter_raw, skip_gain):
    seq_count = lax.axis_size("seq")
    key_f = key_input[0].astype(jnp.float32)
    value_f = value_input[0].astype(jnp.float32)
    out_f = grad_output[0].astype(jnp.float32)
    mixed = key_f * value_f
    gated = out_f * query_gate[0].astype(jnp.float32)
    tokens, channels = mixed.shape
    seq_length = tokens * seq_count
    full_length = 2 * seq_length
    inverse_scale = 1.0 / full_length
    filter_taps = filter_raw.astype(jnp.float32) * seq_length ** (-0.5)
    freq_one = jnp.arange(2 * seq_count, dtype=jnp.int32)
    block_index = jnp.arange(seq_count, dtype=jnp.int32)
    offset_index = jnp.arange(tokens, dtype=jnp.int32)
    cos_one, sin_one = angle_table(freq_one, block_index, 2 * seq_count)
    cos_inv, sin_inv = angle_table(block_index, freq_one, 2 * seq_count)
    cos_two, sin_two = angle_table(offset_index, offset_index, tokens)
    local_width = channels // seq_count
    arrived = (
        lax.all_to_all(mixed.T, "seq", split_axis=0, concat_axis=1, tiled=True),
        lax.all_to_all(gated.T, "seq", split_axis=0, concat_axis=1, tiled=True),
        lax.all_to_all(filter_taps.T, "seq", split_axis=0, concat_axis=1, tiled=True),
    )
    cos_tw, sin_tw = angle_table(freq_one, offset_index, full_length)
    spectra = []
    for line_data in arrived:
        lines = line_data.reshape(local_width, seq_count, tokens)
        real_part, imag_part = rotate("kn,cnm->ckm", cos_one, sin_one, -1.0, lines, None, True)
        real_part, imag_part = twist(cos_tw, sin_tw, -1.0, real_part, imag_part)
        spectra.append(rotate("jm,ckm->ckj", cos_two, sin_two, -1.0, real_part, imag_part, True))
    packed_real, packed_imag, corr_real, corr_imag = spectral_terms(
        spectra[0][0], spectra[0][1], spectra[1][0], spectra[1][1], spectra[2][0], spectra[2][1]
    )
    pr_mid, pi_mid = rotate("mj,ckj->ckm", cos_two, sin_two, 1.0, packed_real, packed_imag, True)
    pr_mid, pi_mid = twist(cos_tw, sin_tw, 1.0, pr_mid, pi_mid)
    cr_mid, ci_mid = rotate("mj,ckj->ckm", cos_two, sin_two, 1.0, corr_real, corr_imag, True)
    cr_mid, ci_mid = twist(cos_tw, sin_tw, 1.0, cr_mid, ci_mid)
    conv_lines, back_lines = rotate("nk,ckm->cnm", cos_inv, sin_inv, 1.0, pr_mid, pi_mid, True)
    corr_lines = rotate("nk,ckm->cnm", cos_inv, sin_inv, 1.0, cr_mid, ci_mid, False)[0]
    conv_lines = (conv_lines * inverse_scale).reshape(local_width, seq_length)
    back_lines = (back_lines * inverse_scale).reshape(local_width, seq_length)
    corr_lines = (corr_lines * inverse_scale).reshape(local_width, seq_length)
    returned = (
        lax.all_to_all(conv_lines, "seq", split_axis=1, concat_axis=0, tiled=True),
        lax.all_to_all(back_lines, "seq", split_axis=1, concat_axis=0, tiled=True),
        lax.all_to_all(corr_lines, "seq", split_axis=1, concat_axis=0, tiled=True),
    )
    conv_time = returned[0].T
    back_time = returned[1].T
    corr_time = returned[2].T
    conv_full = conv_time + skip_gain * mixed
    back_full = back_time + skip_gain * gated
    grad_query = (out_f * conv_full).astype(jnp.bfloat16)[None]
    grad_key = (back_full * value_f).astype(jnp.bfloat16)[None]
    grad_value = (back_full * key_f).astype(jnp.bfloat16)[None]
    grad_filter = lax.psum_scatter(
        corr_time * seq_length ** (-0.5), "ch", scatter_dimension=1, tiled=True
    )
    return (grad_query, grad_key, grad_value, grad_filter)


LANES = 128
VMEM_LIMIT = 60 * 1024 * 1024


def times_root(pair, turn, size):
    real, imag = pair
    turn %= size
    if turn == 0:
        return pair
    if 4 * turn == size:
        return (-imag, real)
    if 2 * turn == size:
        return (-real, -imag)
    if 4 * turn == 3 * size:
        return (imag, -real)
    cosine = math.cos(2.0 * math.pi * turn / size)
    sine = math.sin(2.0 * math.pi * turn / size)
    return (real * cosine - imag * sine, real * sine + imag * cosine)


def complex_dft(values, sense):
    size = len(values)
    if size == 1:
        return values
    even = complex_dft(values[0::2], sense)
    odd = complex_dft(values[1::2], sense)
    low, high = [], []
    for k in range(size // 2):
        er, ei = even[k]
        tr, ti = times_root(odd[k], sense * k, size)
        low.append((er + tr, ei + ti))
        high.append((er - tr, ei - ti))
    return low + high


def half_spectrum(values, size):
    if size == 2:
        return [(values[0] + values[1], None), (values[0] - values[1], None)]
    half, quarter = size // 2, size // 4
    if len(values) == half:
        total, difference = values, values
    else:
        total = [values[n] + values[n + half] for n in range(half)]
        difference = [values[n] - values[n + half] for n in range(half)]
    out = [None] * (half + 1)
    out[0::2] = half_spectrum(total, half)
    turned = [times_root((difference[n], -difference[n + quarter]), -n, size) for n in range(quarter)]
    for index, (real, imag) in enumerate(complex_dft(turned, -1)):
        k = 1 + 4 * index
        if k <= half:
            out[k] = (real, imag)
        else:
            out[size - k] = (real, -imag)
    return out


def real_from_half(terms, size, first_half):
    if size == 2:
        return [terms[0][0] + terms[1][0], terms[0][0] - terms[1][0]]
    half, quarter = size // 2, size // 4
    even = real_from_half(terms[0::2], half, False)
    chosen = []
    for index in range(quarter):
        k = 1 + 4 * index
        if k <= half:
            chosen.append(terms[k])
        else:
            real, imag = terms[size - k]
            chosen.append((real, -imag))
    turned = [times_root(pair, n, size) for n, pair in enumerate(complex_dft(chosen, 1))]
    odd = [pair[0] for pair in turned] + [-pair[1] for pair in turned]
    out = [even[n] + odd[n] for n in range(half)]
    if first_half:
        return out
    return out + [even[n] - odd[n] for n in range(half)]


def split_bf16(value):
    high = value.astype(jnp.bfloat16)
    return high, (value - high.astype(jnp.float32)).astype(jnp.bfloat16)


def three_dot(table_high, table_low, value):
    high, low = split_bf16(value)
    dot = lambda a, b: jnp.dot(a, b, preferred_element_type=jnp.float32)
    return dot(table_high, high) + (dot(table_high, low) + dot(table_low, high))


def far_first(seq_count, ch_count):
    steps = sorted(range(seq_count), key=lambda step: abs(2 * step - seq_count))
    return [(step, turn) for step in steps for turn in range(ch_count) if step or turn]


def partner_of(step, turn, seq_count, ch_count, me_seq, me_ch):
    return {"seq": lax.rem(me_seq + step, seq_count), "ch": lax.rem(me_ch + turn, ch_count)}


def left_mask(shape):
    return lax.broadcasted_iota(jnp.int32, shape, 1) < LANES // 2


def swap_halves(value):
    return pltpu.roll(value, LANES // 2, 1)


def greet_all(seq_count, ch_count, me_seq, me_ch):
    barrier = pltpu.get_barrier_semaphore()
    for step, turn in far_first(seq_count, ch_count):
        pl.semaphore_signal(barrier, inc=1, device_id=partner_of(step, turn, seq_count, ch_count, me_seq, me_ch), device_id_type=pl.DeviceIdType.MESH)
    return barrier


def exchange(sends, turn, seq_count, ch_count, me_seq, me_ch):
    copies = []
    for step, at in far_first(seq_count, ch_count):
        if at != turn:
            continue
        partner = partner_of(step, turn, seq_count, ch_count, me_seq, me_ch)
        for source, target, send_sem, recv_sem, per_seq in sends:
            if per_seq:
                give, take, slot = partner["seq"], me_seq, step
            else:
                give, take, slot = partner["ch"] * seq_count + partner["seq"], me_ch * seq_count + me_seq, step * ch_count + turn
            copy = pltpu.make_async_remote_copy(
                src_ref=source.at[give],
                dst_ref=target.at[take],
                send_sem=send_sem.at[slot],
                recv_sem=recv_sem.at[slot],
                device_id=partner,
                device_id_type=pl.DeviceIdType.MESH,
            )
            copy.start()
            copies.append(copy)
    return copies


def layer_kernel(
    seq_count, ch_count,
    query_ref, key_ref, value_ref, out_ref, filter_ref, skip_ref, fwd_ref, inv_ref, tw_ref,
    gq_ref, gk_ref, gv_ref, gf_ref,
    send, taps_send, recv, taps_recv, result, corr_result, back_recv, corr_recv,
    spec, taps_spec, corr_spec, taps_scr, corr_scr, tw_scr,
    send_sem, recv_sem, taps_send_sem, taps_recv_sem, back_send_sem, back_recv_sem, corr_send_sem, corr_recv_sem,
):
    me_seq, me_ch = lax.axis_index("seq"), lax.axis_index("ch")
    where_am_i = (seq_count, ch_count, me_seq, me_ch)
    tokens, channels = key_ref.shape
    half_tokens = tokens // 2
    size = 2 * seq_count
    scale = (seq_count * tokens) ** -0.5
    own = me_ch * (channels // ch_count)
    mine = me_ch * seq_count + me_seq
    barrier = greet_all(*where_am_i)

    def prepare_taps(group, carry):
        lanes = pl.ds(pl.multiple_of(own + group * LANES, LANES), LANES)
        taps = filter_ref[:, lanes].astype(jnp.float32) * scale
        top, bottom = taps[:half_tokens], taps[half_tokens:]
        left = left_mask(top.shape)
        taps_send[2 * group] = jnp.where(left, top, swap_halves(bottom))
        taps_send[2 * group + 1] = jnp.where(left, swap_halves(top), bottom)
        return carry

    lax.fori_loop(0, seq_count // 2, prepare_taps, 0)

    def prepare(group, carry):
        lanes = pl.ds(pl.multiple_of(group * LANES, LANES), LANES)
        mixed = key_ref[:, lanes].astype(jnp.float32) * value_ref[:, lanes].astype(jnp.float32)
        gated = out_ref[:, lanes].astype(jnp.float32) * query_ref[:, lanes].astype(jnp.float32)
        left = left_mask(mixed.shape)
        send[2 * group] = jnp.where(left, mixed, swap_halves(gated))
        send[2 * group + 1] = jnp.where(left, swap_halves(mixed), gated)
        return carry

    lax.fori_loop(0, seq_count, prepare, 0)
    pl.semaphore_wait(barrier, len(far_first(seq_count, ch_count)))
    arriving = [exchange([(taps_send, taps_recv, taps_send_sem, taps_recv_sem, True), (send, recv, send_sem, recv_sem, False)], 0, *where_am_i)]
    arriving.append(exchange([(send, recv, send_sem, recv_sem, False)], 1, *where_am_i))
    recv[mine] = send[mine]
    taps_recv[me_seq] = taps_send[me_seq]
    for k in range(seq_count + 1):
        for part in range(2):
            tw_scr[k, part] = jnp.broadcast_to(tw_ref[part, :, k:k + 1], (tokens, LANES))
    for copy in arriving[0]:
        copy.wait_recv()

    def spread_taps(block, carry):
        packed = taps_recv[block]
        rolled = swap_halves(packed)
        left = left_mask(packed.shape)
        taps_scr[block, :half_tokens, :] = jnp.where(left, packed, rolled)
        taps_scr[block, half_tokens:, :] = jnp.where(left, rolled, packed)
        return carry

    lax.fori_loop(0, seq_count, spread_taps, 0)

    def analyse(load, target):
        def body(chunk, carry):
            rows = pl.ds(pl.multiple_of(chunk * 8, 8), 8)
            for k, (real, imag) in enumerate(half_spectrum([load(n, rows) for n in range(seq_count)], size)):
                target[k, 0, rows, :] = real
                target[k, 1, rows, :] = jnp.zeros_like(real) if imag is None else imag
            return carry

        lax.fori_loop(0, tokens // 8, body, 0)

    def synthesise(source, store):
        def body(chunk, carry):
            rows = pl.ds(pl.multiple_of(chunk * 8, 8), 8)
            terms = [(source[k, 0, rows, :], source[k, 1, rows, :]) for k in range(seq_count + 1)]
            for n, value in enumerate(real_from_half(terms, size, True)):
                store(n, rows, value)
            return carry

        lax.fori_loop(0, tokens // 8, body, 0)

    def across(tables, real, imag):
        both = three_dot(tables[0], tables[1], jnp.concatenate([real, imag], axis=0))
        return both[:tokens], both[tokens:]

    def convolve(batch, first):
        base = batch * seq_count
        analyse(lambda n, rows: recv[base + n, rows, :], spec)
        if first:
            analyse(lambda n, rows: taps_scr[n, rows, :], taps_spec)
        forward = (fwd_ref[0], fwd_ref[1])
        inverse = (inv_ref[0], inv_ref[1])

        def middle(k, carry):
            cosine, sine = tw_scr[k, 0], tw_scr[k, 1]
            real, imag = spec[k, 0], spec[k, 1]
            real, imag = real * cosine + imag * sine, imag * cosine - real * sine
            if first:
                tr, ti = taps_spec[k, 0], taps_spec[k, 1]
                tr, ti = tr * cosine + ti * sine, ti * cosine - tr * sine
                real, imag = across(forward, jnp.concatenate([real, tr], axis=1), jnp.concatenate([imag, ti], axis=1))
                h_r, h_i = real[:, LANES:], imag[:, LANES:]
                a_r, a_i = real[:, :LANES], imag[:, :LANES]
                h_i = jnp.where(left_mask(h_i.shape), h_i, -h_i)
                taps_spec[k, 0], taps_spec[k, 1] = h_r, h_i
            else:
                a_r, a_i = across(forward, real, imag)
                h_r, h_i = taps_spec[k, 0], taps_spec[k, 1]
            g_r, g_i = swap_halves(a_r), swap_halves(a_i)
            c_r, c_i = a_r * g_r + a_i * g_i, a_r * g_i - a_i * g_r
            p_r, p_i = a_r * h_r - a_i * h_i, a_r * h_i + a_i * h_r
            weight = jnp.where((k == 0) | (k == seq_count), 0.5 / (seq_count * tokens), 1.0 / (seq_count * tokens))
            cosine, sine = cosine * weight, sine * weight
            if first:
                corr_spec[k, 0], corr_spec[k, 1] = c_r, c_i
                br, bi = across(inverse, p_r, p_i)
            else:
                c_r, c_i = c_r + corr_spec[k, 0], c_i + corr_spec[k, 1]
                both_r, both_i = across(inverse, jnp.concatenate([p_r, c_r], axis=1), jnp.concatenate([p_i, c_i], axis=1))
                br, bi = both_r[:, :LANES], both_i[:, :LANES]
                cr, ci = both_r[:, LANES:], both_i[:, LANES:]
                corr_spec[k, 0] = cr * cosine - ci * sine
                corr_spec[k, 1] = ci * cosine + cr * sine
            spec[k, 0] = br * cosine - bi * sine
            spec[k, 1] = bi * cosine + br * sine
            return carry

        lax.fori_loop(0, seq_count + 1, middle, 0)

        def store(n, rows, value):
            result[base + n, rows, :] = value

        synthesise(spec, store)

    returning = [(result, back_recv, back_send_sem, back_recv_sem, False)]
    convolve(me_ch, True)
    leaving = exchange(returning, 0, *where_am_i)
    for copy in arriving[1]:
        copy.wait_recv()
    convolve(lax.rem(me_ch + 1, ch_count), False)
    leaving += exchange(returning, 1, *where_am_i)

    def store_corr(n, rows, value):
        corr_scr[n, rows, :] = value

    synthesise(corr_spec, store_corr)

    def gather_corr(block, carry):
        top = corr_scr[block, :half_tokens, :]
        bottom = swap_halves(corr_scr[block, half_tokens:, :])
        corr_result[block] = jnp.where(left_mask(top.shape), top, bottom) * scale
        return carry

    lax.fori_loop(0, seq_count, gather_corr, 0)
    last = exchange([(corr_result, corr_recv, corr_send_sem, corr_recv_sem, True)], 0, *where_am_i)
    back_recv[mine] = result[mine]
    corr_recv[me_seq] = corr_result[me_seq]
    for copy in leaving:
        copy.wait_recv()

    def finish(group, carry):
        lanes = pl.ds(pl.multiple_of(group * LANES, LANES), LANES)
        query_f = query_ref[:, lanes].astype(jnp.float32)
        key_f = key_ref[:, lanes].astype(jnp.float32)
        value_f = value_ref[:, lanes].astype(jnp.float32)
        out_f = out_ref[:, lanes].astype(jnp.float32)
        one, two = back_recv[2 * group], back_recv[2 * group + 1]
        left = left_mask(one.shape)
        skip = skip_ref[:, lanes]
        conv = jnp.where(left, one, swap_halves(two)) + skip * (key_f * value_f)
        back = jnp.where(left, swap_halves(one), two) + skip * (out_f * query_f)
        gq_ref[:, lanes] = (out_f * conv).astype(jnp.bfloat16)
        gk_ref[:, lanes] = (back * value_f).astype(jnp.bfloat16)
        gv_ref[:, lanes] = (back * key_f).astype(jnp.bfloat16)
        return carry

    lax.fori_loop(0, seq_count, finish, 0)
    for copy in last:
        copy.wait_recv()

    def finish_corr(group, carry):
        lanes = pl.ds(pl.multiple_of(group * LANES, LANES), LANES)
        one, two = corr_recv[2 * group], corr_recv[2 * group + 1]
        left = left_mask(one.shape)
        gf_ref[:half_tokens, lanes] = jnp.where(left, one, swap_halves(two))
        gf_ref[half_tokens:, lanes] = jnp.where(left, swap_halves(one), two)
        return carry

    lax.fori_loop(0, seq_count // 2, finish_corr, 0)
    for copy in arriving[0] + arriving[1] + leaving + last:
        copy.wait_send()


def tables(seq_count, tokens):
    index = np.arange(tokens)
    angle = 2.0 * np.pi / tokens * (index[:, None] * index[None, :] % tokens)
    cosine, sine = np.cos(angle), np.sin(angle)
    forward = np.block([[cosine, sine], [-sine, cosine]]).astype(np.float32)
    inverse = np.block([[cosine, -sine], [sine, cosine]]).astype(np.float32)

    def pieces(table):
        table = jnp.asarray(table)
        return jnp.stack(split_bf16(table))

    turn = 2.0 * np.pi / (2 * seq_count * tokens) * (np.arange(seq_count + 1)[:, None] * index[None, :])
    twiddle = jnp.asarray(np.stack([np.cos(turn).T, np.sin(turn).T]).astype(np.float32))
    return pieces(forward), pieces(inverse), twiddle


def fast_shards(query_gate, key_input, value_input, grad_output, filter_raw, skip_gain):
    seq_count, ch_count = lax.axis_size("seq"), lax.axis_size("ch")
    owners = seq_count * ch_count
    _, tokens, channels = key_input.shape
    vmem = pl.BlockSpec(memory_space=pltpu.VMEM)
    chunks = pltpu.VMEM((owners, tokens, LANES), jnp.float32)
    halves = pltpu.VMEM((seq_count, tokens // 2, LANES), jnp.float32)
    spectrum = pltpu.VMEM((seq_count + 1, 2, tokens, LANES), jnp.float32)
    lines = pltpu.VMEM((seq_count, tokens, LANES), jnp.float32)
    per_owner = pltpu.SemaphoreType.DMA((owners,))
    per_seq = pltpu.SemaphoreType.DMA((seq_count,))
    grads = pl.pallas_call(
        lambda *refs: layer_kernel(seq_count, ch_count, *refs),
        in_specs=[vmem] * 9,
        out_specs=[vmem] * 4,
        out_shape=[jax.ShapeDtypeStruct((tokens, channels), jnp.bfloat16)] * 3
        + [jax.ShapeDtypeStruct((tokens, channels // ch_count), jnp.float32)],
        scratch_shapes=[
            chunks, halves, chunks, halves, chunks, halves, chunks, halves,
            spectrum, spectrum, spectrum, lines, lines, spectrum,
            per_owner, per_owner, per_seq, per_seq, per_owner, per_owner, per_seq, per_seq,
        ],
        compiler_params=pltpu.CompilerParams(vmem_limit_bytes=VMEM_LIMIT, collective_id=0, has_side_effects=True),
        name="layer",
    )(query_gate[0], key_input[0], value_input[0], grad_output[0], filter_raw, skip_gain[None], *tables(seq_count, tokens))
    return (grads[0][None], grads[1][None], grads[2][None], grads[3])


def solution(mesh):
    in_specs = (
        P("ch", "seq", None),
        P("ch", "seq", None),
        P("ch", "seq", None),
        P("ch", "seq", None),
        P("seq", None),
        P(),
    )
    out_specs = (P("ch", "seq", None), P("ch", "seq", None), P("ch", "seq", None), P("seq", "ch"))

    def body(*arrays):
        seq_count, ch_count = mesh.shape["seq"], mesh.shape["ch"]
        _, tokens, channels = arrays[0].shape
        fits = ch_count == 2 and tokens == LANES and channels == seq_count * LANES and seq_count <= 32
        return (fast_shards if fits else shards)(*arrays)

    return jax.shard_map(body, mesh=mesh, in_specs=in_specs, out_specs=out_specs, check_vma=False)
```

profile of v0, /device:TPU:0, one launch (start us, length us, event | category | flops | bytes accessed | tf_op | source)
XLA Modules:
  0.0 131.3 jit_solution(14718458291810674703)
XLA Ops:
  0.6 125.5 %layer.1 = (bf16[128,2048]{1,0:T(8,128)(2,1)}, bf16[128,2048]{1,0:T(8,128)(2,1)}, bf16[128,2048]{1,0:T(8,128)(2,1)}, f32[128,1024]{1,0:T(8,128)}) custom-call(bf16[128,2048]{1,0:T(8,128)(2,1)} %bitcast.8, bf16[128,2048]{1,0:T(8,128)(2,1)} %bitcast.9, bf16[128,2048]{1,0:T(8,128)(2,1)} %bitcast.10, bf16[128,2048]{1,0:T(8,128)(2,1)} %bitcast.11, ...), custom_call_target="tpu_custom_call" | custom-call | tf_op jit(solution)/shard_map/layer/pallas_call | solution.py:474
  126.1 0.0 copy-start.2
  126.1 1.9 %copy.17 = bf16[1,128,2048]{2,1,0:T(8,128)(2,1)} copy(bf16[1,128,2048]{2,1,0:T(8,128)(2,1)} %bitcast.14) | data formatting | bytes 1048576
  128.1 0.0 copy-done.2
  128.1 0.0 copy-start.1
  128.1 0.8 copy.18
  128.9 0.4 copy-done.1
  129.3 0.0 copy-start
  129.3 0.8 copy.19
  130.1 0.4 copy-done
  130.5 0.8 copy.20
Async XLA Ops:
  126.1 2.0 %copy-start.2 = (bf16[128,2048]{1,0:T(8,128)(2,1)S(1)}, bf16[128,2048]{1,0:T(8,128)(2,1)}, u32[]{:S(2)}) copy-start(bf16[128,2048]{1,0:T(8,128)(2,1)} %get-tuple-element.9) | copy-start | bytes 1572868
  128.1 1.2 copy-start.1
  129.3 1.2 copy-start
where the time goes:
time: 132 us; the launch traced here: 131 us
  Pallas kernels  125 us (95%)
  local copies, waits for them, and re-layouts  5.19 us (4%)
    pallas_call x1, Pallas kernels, fast_shards(): pl.pallas_call(lambda *refs: layer_kernel(seq_count, ch_count, *refs), in...  125 us
    unnamed x10, local copies, waits for them, and re-layouts  5.19 us

commit v1 on v0

--- a/solution.py
+++ b/solution.py
@@ -281,6 +281,9 @@
 
     lax.fori_loop(0, seq_count // 2, prepare_taps, 0)
 
+    pl.semaphore_wait(barrier, len(far_first(seq_count, ch_count)))
+    arriving = [exchange([(taps_send, taps_recv, taps_send_sem, taps_recv_sem, True)], 0, *where_am_i)]
+
     def prepare(group, carry):
         lanes = pl.ds(pl.multiple_of(group * LANES, LANES), LANES)
         mixed = key_ref[:, lanes].astype(jnp.float32) * value_ref[:, lanes].astype(jnp.float32)
@@ -290,9 +293,12 @@
         send[2 * group + 1] = jnp.where(left, swap_halves(mixed), gated)
         return carry
 
-    lax.fori_loop(0, seq_count, prepare, 0)
-    pl.semaphore_wait(barrier, len(far_first(seq_count, ch_count)))
-    arriving = [exchange([(taps_send, taps_recv, taps_send_sem, taps_recv_sem, True), (send, recv, send_sem, recv_sem, False)], 0, *where_am_i)]
+    groups = seq_count // ch_count
+    first_group = me_ch * groups
+    other_group = lax.rem(me_ch + 1, ch_count) * groups
+    lax.fori_loop(first_group, first_group + groups, prepare, 0)
+    arriving[0] += exchange([(send, recv, send_sem, recv_sem, False)], 0, *where_am_i)
+    lax.fori_loop(other_group, other_group + groups, prepare, 0)
     arriving.append(exchange([(send, recv, send_sem, recv_sem, False)], 1, *where_am_i))
     recv[mine] = send[mine]
     taps_recv[me_seq] = taps_send[me_seq]
@@ -387,11 +393,11 @@
 
     returning = [(result, back_recv, back_send_sem, back_recv_sem, False)]
     convolve(me_ch, True)
-    leaving = exchange(returning, 0, *where_am_i)
+    leaving = [exchange(returning, 0, *where_am_i)]
     for copy in arriving[1]:
         copy.wait_recv()
     convolve(lax.rem(me_ch + 1, ch_count), False)
-    leaving += exchange(returning, 1, *where_am_i)
+    leaving.append(exchange(returning, 1, *where_am_i))
 
     def store_corr(n, rows, value):
         corr_scr[n, rows, :] = value
@@ -408,8 +414,6 @@
     last = exchange([(corr_result, corr_recv, corr_send_sem, corr_recv_sem, True)], 0, *where_am_i)
     back_recv[mine] = result[mine]
     corr_recv[me_seq] = corr_result[me_seq]
-    for copy in leaving:
-        copy.wait_recv()
 
     def finish(group, carry):
         lanes = pl.ds(pl.multiple_of(group * LANES, LANES), LANES)
@@ -427,7 +431,12 @@
         gv_ref[:, lanes] = (back * key_f).astype(jnp.bfloat16)
         return carry
 
-    lax.fori_loop(0, seq_count, finish, 0)
+    for copy in leaving[0]:
+        copy.wait_recv()
+    lax.fori_loop(first_group, first_group + groups, finish, 0)
+    for copy in leaving[1]:
+        copy.wait_recv()
+    lax.fori_loop(other_group, other_group + groups, finish, 0)
     for copy in last:
         copy.wait_recv()
 
@@ -440,7 +449,7 @@
         return carry
 
     lax.fori_loop(0, seq_count // 2, finish_corr, 0)
-    for copy in arriving[0] + arriving[1] + leaving + last:
+    for copy in arriving[0] + arriving[1] + leaving[0] + leaving[1] + last:
         copy.wait_send()
 
 

time: 132 us -> 131 us (level)
  no operation moved by 1% of the time
where the time goes in v1:
time: 131 us
  Pallas kernels  125 us (95%)
  local copies, waits for them, and re-layouts  5.19 us (4%)
    pallas_call x1, Pallas kernels, fast_shards(): pl.pallas_call(lambda *refs: layer_kernel(seq_count, ch_count, *refs), in...  125 us
    unnamed x10, local copies, waits for them, and re-layouts  5.19 us

profile of v1, /device:TPU:0, one launch (start us, length us, event | category | flops | bytes accessed | tf_op | source)
XLA Modules:
  0.0 130.6 jit_solution(4383641437918287933)
XLA Ops:
  0.6 124.7 %layer.1 = (bf16[128,2048]{1,0:T(8,128)(2,1)}, bf16[128,2048]{1,0:T(8,128)(2,1)}, bf16[128,2048]{1,0:T(8,128)(2,1)}, f32[128,1024]{1,0:T(8,128)}) custom-call(bf16[128,2048]{1,0:T(8,128)(2,1)} %bitcast.8, bf16[128,2048]{1,0:T(8,128)(2,1)} %bitcast.9, bf16[128,2048]{1,0:T(8,128)(2,1)} %bitcast.10, bf16[128,2048]{1,0:T(8,128)(2,1)} %bitcast.11, ...), custom_call_target="tpu_custom_call" | custom-call | tf_op jit(solution)/shard_map/layer/pallas_call | solution.py:483
  125.4 0.0 copy-start.2
  125.4 1.9 %copy.17 = bf16[1,128,2048]{2,1,0:T(8,128)(2,1)} copy(bf16[1,128,2048]{2,1,0:T(8,128)(2,1)} %bitcast.14) | data formatting | bytes 1048576
  127.3 0.0 copy-done.2
  127.3 0.0 copy-start.1
  127.3 0.8 copy.18
  128.1 0.4 copy-done.1
  128.6 0.0 copy-start
  128.6 0.8 copy.19
  129.4 0.4 copy-done
  129.8 0.8 copy.20
Async XLA Ops:
  125.4 2.0 %copy-start.2 = (bf16[128,2048]{1,0:T(8,128)(2,1)S(1)}, bf16[128,2048]{1,0:T(8,128)(2,1)}, u32[]{:S(2)}) copy-start(bf16[128,2048]{1,0:T(8,128)(2,1)} %get-tuple-element.9) | copy-start | bytes 1572868
  127.3 1.2 copy-start.1
  128.6 1.2 copy-start
